TPU v7x, 32 devices: a whole 2x2x4 slice. The times are simulated.
32 devices in a mesh: fsdp: 4 (over y, x), tp: 2 (over core), rep: 4 (over z).
Axes of the slice: x: 2, y: 2, z: 4, core: 2. Of those that a mesh axis runs over, the one named last changes fastest.
Arguments:
- tokens: bfloat16 [4096, 5120], P('fsdp', 'rep'), may hold values from -6 to 6
- ref_qkv: bfloat16 [5120, 7168], P(('rep', 'fsdp'), 'tp'), may hold values from -0.078125 to 0.078125
- ref_bias: float32 [7168], P('tp'), may hold values from -9 to 9
- segment_ids: int32 [4, 1024], P('fsdp'), may hold values from 0 to 7, never falling along the last dimension, each value on 1 to 512 neighbouring positions
- policy_key: bfloat16 [5120, 1024], P(('rep', 'fsdp'), 'tp'), may hold values from -0.078125 to 0.078125
Outputs:
- context: bfloat16 [4096, 5120], P(('fsdp', 'rep'), 'tp')
- policy_key_tp: bfloat16 [5120, 1024], P(None, 'tp')
All inputs are finite; a program needn't handle non-finite values.
Results may differ from a plain program's by a relative error of at most 0.0093.
Values may be sent and summed in bfloat16 or wider, within the bound.
A program may use at most 128 MiB of HBM per device.

v0:
```python
import jax
import jax.numpy as jnp
from jax import lax
from jax.sharding import PartitionSpec as P

QH = 40
KVH = 8
HD = 128


def positions_of(seg):
    count = seg.shape[0]
    index = jnp.arange(count, dtype=jnp.int32)
    starts = jnp.concatenate([jnp.ones((1,), bool), seg[1:] != seg[:-1]])
    first = lax.cummax(jnp.where(starts, index, 0), axis=0)
    return index - first


def rotary(values, pos):
    half = values.shape[-1] // 2
    freq = 1000000.0 ** (-2.0 * jnp.arange(half, dtype=jnp.float32) / values.shape[-1])
    angle = pos.astype(jnp.float32)[:, None] * freq[None, :]
    shape = (values.shape[0],) + (1,) * (values.ndim - 2) + (half,)
    cosine = jnp.cos(angle).reshape(shape)
    sine = jnp.sin(angle).reshape(shape)
    first = values[..., :half]
    second = values[..., half:]
    return jnp.concatenate(
        [first * cosine - second * sine, second * cosine + first * sine], axis=-1
    )


def per_device(tokens, ref_qkv, ref_bias, segment_ids, policy_key):
    share = QH // KVH
    rows = tokens.shape[0]
    columns = ref_qkv.shape[1]
    groups = columns // ((share + 2) * HD)
    replicas = lax.axis_size("rep")
    mine = rows // replicas
    rank = lax.axis_index("rep")
    partial_value = jnp.dot(
        tokens,
        lax.all_gather(ref_qkv, "fsdp", axis=0, tiled=True),
        preferred_element_type=jnp.float32,
    )
    partial_value = partial_value.reshape(rows, groups, share + 2, HD)
    bias = ref_bias.reshape(groups, share + 2, HD)
    seg = segment_ids[0]
    pos = positions_of(seg)
    start = rank * mine
    my_pos = lax.dynamic_slice_in_dim(pos, start, mine, 0)
    summed = lax.psum_scatter(partial_value, "rep", scatter_dimension=0, tiled=True) + bias[None]
    query = rotary(summed[:, :, :share], my_pos).astype(jnp.bfloat16)
    my_keys = rotary(summed[:, :, share], my_pos).astype(jnp.bfloat16)
    my_vals = summed[:, :, share + 1].astype(jnp.bfloat16)
    keys, vals = (
        lax.all_gather(my_keys, "rep", axis=0, tiled=True),
        lax.all_gather(my_vals, "rep", axis=0, tiled=True),
    )
    scores = jnp.einsum(
        "qhgd,khd->hgqk", query, keys, preferred_element_type=jnp.float32
    ) / jnp.sqrt(jnp.float32(HD))
    query_index = start + jnp.arange(mine, dtype=jnp.int32)
    key_index = jnp.arange(rows, dtype=jnp.int32)
    my_seg = lax.dynamic_slice_in_dim(seg, start, mine, 0)
    allowed = (my_seg[:, None] == seg[None, :]) & (key_index[None, :] <= query_index[:, None])
    scores = jnp.where(allowed[None, None], scores, -1e30)
    top = jnp.max(scores, axis=-1, keepdims=True)
    expo = jnp.exp(scores - top)
    weights = (expo / jnp.sum(expo, axis=-1, keepdims=True)).astype(jnp.bfloat16)
    context = jnp.einsum("hgqk,khd->qhgd", weights, vals, preferred_element_type=jnp.float32)
    context = context.astype(jnp.bfloat16).reshape(mine, groups * share * HD)
    inner = lax.all_gather(policy_key, "rep", axis=0, tiled=True)
    outer = lax.all_gather(inner, "fsdp", axis=0, tiled=True)
    blocks = policy_key.shape[0]
    shards = outer.shape[0] // (blocks * replicas)
    whole = (
        outer.reshape(shards, replicas, blocks, outer.shape[1])
        .transpose(1, 0, 2, 3)
        .reshape(outer.shape)
    )
    return (context, whole)


def solution(mesh):
    in_specs = (
        P("fsdp", "rep"),
        P(("rep", "fsdp"), "tp"),
        P("tp"),
        P("fsdp", None),
        P(("rep", "fsdp"), "tp"),
    )
    out_specs = (P(("fsdp", "rep"), "tp"), P(None, "tp"))
    return jax.shard_map(
        per_device, mesh=mesh, in_specs=in_specs, out_specs=out_specs, check_vma=False
    )
```

profile of v0, /device:TPU:0, one launch (start us, length us, event | category | flops | bytes accessed | tf_op | source)
XLA Modules:
  0.0 530.3 jit_solution(14261949471272091948)
XLA Ops:
  7.2 0.0 copy-start
  7.2 0.0 all-gather.7.cloned.1.call-start
  7.2 0.7 all-gather.7.cloned.1.call-update
  7.9 0.0 all-gather.11.cloned.1.call-start
  8.0 0.7 all-gather.11.cloned.1.call-update
  8.7 0.0 reduce-scatter.2.cloned.1.call-start
  8.7 97.9 %all-gather.7.cloned.1.call-done = bf16[1280,3584]{1,0:T(8,128)(2,1)} async-done(((bf16[320,3584]{1,0:T(8,128)(2,1)}), bf16[1280,3584]{1,0:T(8,128)(2,1)}) %all-gather.7.cloned.1.call-update) | async-done | bytes 9175056 | tf_op jit(solution)/shard_map/all_gather | solution.py:43
  106.6 0.0 copy-done
  106.6 15.2 %fusion.29 = f32[1024,3584]{0,1:T(8,128)} fusion(bf16[1024,1280]{1,0:T(8,128)(2,1)S(1)} %copy-done, bf16[1280,3584]{1,0:T(8,128)(2,1)} %all-gather.7.cloned.1.call-done), kind=kOutput, calls=%fused_computation.42 | convolution fusion | flops 9395240960 | bytes 26476544 | tf_op jit(solution)/shard_map/dot_general | solution.py:41
  121.8 15.2 %copy.13 = f32[1024,4,7,128]{3,0,2,1:T(8,128)} copy(f32[1024,4,7,128]{0,3,2,1:T(8,128)} %bitcast.53) | data formatting | bytes 29360128 | tf_op jit(solution)/shard_map/reshape | solution.py:46
  137.0 0.0 copy-start.4
  137.0 0.0 copy-start.3
  137.0 0.0 reduce-scatter.2.cloned.1.call-update
  137.0 0.0 all-gather.13.cloned.1.call-start
  137.1 3.6 all-gather.11.cloned.1.call-done
  140.7 0.0 all-gather.13.cloned.1.call-update
  140.7 0.0 all-gather.9.cloned.1.call-start
  140.8 0.0 copy-done.4
  140.8 0.0 copy-done.3
  140.8 0.1 compare_reduce_fusion
  140.9 0.1 add_select_fusion
  141.0 0.3 reduce-window.9
  141.3 0.1 slice.42
  141.4 0.1 slice_reduce_fusion
  141.5 0.1 bitcast_subtract_fusion
  141.6 0.1 dynamic-slice_convert_fusion
  141.7 0.5 multiply_cosine_fusion
  142.2 245.7 %reduce-scatter.2.cloned.1.call-done = f32[256,4,7,128]{3,0,2,1:T(8,128)} async-done(((f32[1024,4,7,128]{3,0,2,1:T(8,128)}), f32[256,4,7,128]{3,0,2,1:T(8,128)}) %reduce-scatter.2.cloned.1.call-update) | async-done | bytes 3670032 | tf_op jit(solution)/shard_map/reduce_scatter | solution.py:52
  387.9 2.5 broadcast_add_fusion
  390.4 0.0 copy-start.2
  390.4 1.8 copy-done.2
  392.2 0.3 subtract_convert_fusion.1
  392.5 0.9 pad_maximum_fusion.1
  393.4 0.0 all-gather.9.cloned.1.call-update
  393.4 0.2 all-gather.15.cloned.1.call-start
  393.6 0.3 fusion.17
  393.9 58.1 %all-gather.13.cloned.1.call-done = bf16[5120,512]{1,0:T(8,128)(2,1)} async-done(((bf16[1280,512]{1,0:T(8,128)(2,1)}), bf16[5120,512]{1,0:T(8,128)(2,1)}) %all-gather.13.cloned.1.call-update) | async-done | bytes 5242896 | tf_op jit(solution)/shard_map/all_gather | solution.py:74
  452.0 5.3 %copy.16 = bf16[4,4,320,512]{3,2,0,1:T(8,128)(2,1)} copy(bf16[4,4,320,512]{3,2,1,0:T(8,128)(2,1)} %bitcast.54) | data formatting | bytes 10485760 | tf_op jit(solution)/shard_map/reshape | solution.py:78
  457.3 1.8 slice.67
  459.1 0.0 all-gather.15.cloned.1.call-update
  459.1 3.7 subtract_convert_fusion
  462.8 19.2 %all-gather.9.cloned.1.call-done = bf16[1024,4,128]{2,0,1:T(8,128)(2,1)} async-done(((bf16[256,4,128]{2,0,1:T(8,128)(2,1)}), bf16[1024,4,128]{2,0,1:T(8,128)(2,1)}) %all-gather.9.cloned.1.call-update) | async-done | bytes 1048592 | tf_op jit(solution)/shard_map/all_gather | solution.py:57
  482.0 12.1 %fusion.24 = (f32[4,5,256]{2,1,0:T(8,128)S(1)}, f32[4,5,256,1024]{2,3,1,0:T(8,128)}) fusion(pred[256,1024]{0,1:T(8,128)(4,1)S(1)} %fusion.17, bf16[1024,4,128]{2,0,1:T(8,128)(2,1)} %all-gather.9.cloned.1.call-done, bf16[256,4,5,64]{3,0,2,1:T(8,128)(2,1)S(1)} %get-tuple-element.7, bf16[256,4,5,64]{3,0,2,1:T(8,128)(2,1)S(1)} %get-tuple-element.6), kind=kOutput, calls=%fused_computation.41 | convolution fusion | flops 1365771264 | bytes 23613440 | tf_op jit(solution)/shard_map/sub | solution.py:69
  494.2 16.7 %all-gather.15.cloned.1.call-done = bf16[1024,4,1,128]{3,0,2,1:T(8,128)(2,1)} async-done(((bf16[256,4,1,128]{3,0,2,1:T(8,128)(2,1)}), bf16[1024,4,1,128]{3,0,2,1:T(8,128)(2,1)}) %all-gather.15.cloned.1.call-update) | async-done | bytes 1048592 | tf_op jit(solution)/shard_map/all_gather | solution.py:58
  510.8 0.0 copy-start.1
  510.8 10.2 %fusion.8 = bf16[4,128,5,256]{3,1,2,0:T(8,128)(2,1)} fusion(f32[4,5,256,1024]{2,3,1,0:T(8,128)} %get-tuple-element.13, f32[4,5,256]{2,1,0:T(8,128)S(1)} %get-tuple-element.12, bf16[1024,4,1,128]{3,0,2,1:T(8,128)(2,1)} %all-gather.15.cloned.1.call-done), kind=kOutput, calls=%fused_computation.13 | convolution fusion | flops 1353318400 | bytes 23351296 | tf_op jit(solution)/shard_map/hgqk,khd->qhgd/dot_general | solution.py:71
  521.0 2.4 copy.17
  523.5 0.0 copy-done.1
  (6 shorter events, 0.1 us)
Async XLA Ops:
  7.2 99.4 %copy-start = (bf16[1024,1280]{1,0:T(8,128)(2,1)S(1)}, bf16[1024,1280]{1,0:T(8,128)(2,1)}, u32[]{:S(2)}) copy-start(bf16[1024,1280]{1,0:T(8,128)(2,1)} %param.5) | copy-start | bytes 7864324
  7.2 99.4 %all-gather.7.cloned.1.call-start = ((), (), s32[]{:S(2)}) async-start(), calls=%async_computation.1 | async-start | bytes 11468800 | tf_op jit(solution)/shard_map/all_gather | solution.py:43
  7.9 132.8 %all-gather.11.cloned.1.call-start = ((), (), s32[]{:S(2)}) async-start(), calls=%async_computation.4 | async-start | bytes 1638400 | tf_op jit(solution)/shard_map/all_gather | solution.py:73
  8.7 379.3 %reduce-scatter.2.cloned.1.call-start = ((), (), s32[]{:S(2)}) async-start(), calls=%async_computation.2 | async-start | bytes 18350080 | tf_op jit(solution)/shard_map/reduce_scatter | solution.py:52
  137.0 3.8 copy-start.4
  137.0 3.8 copy-start.3
  137.0 315.0 %all-gather.13.cloned.1.call-start = ((), (), s32[]{:S(2)}) async-start(), calls=%async_computation.5 | async-start | bytes 6553600 | tf_op jit(solution)/shard_map/all_gather | solution.py:74
  140.7 341.3 %all-gather.9.cloned.1.call-start = ((), (), s32[]{:S(2)}) async-start(), calls=%async_computation.3 | async-start | bytes 1310720 | tf_op jit(solution)/shard_map/all_gather | solution.py:57
  390.4 1.8 copy-start.2
  393.4 117.5 %all-gather.15.cloned.1.call-start = ((), (), s32[]{:S(2)}) async-start(), calls=%async_computation.6 | async-start | bytes 1310720 | tf_op jit(solution)/shard_map/all_gather | solution.py:58
  510.8 12.6 %copy-start.1 = (bf16[1024,1280]{1,0:T(8,128)(2,1)S(1)}, bf16[1024,1280]{1,0:T(8,128)(2,1)}, u32[]{:S(2)}) copy-start(bf16[1024,1280]{1,0:T(8,128)(2,1)} %param.5) | copy-start | bytes 7864324
Sparse Core Ops, SparseCore 0:
  9.8 96.7 all-gather.6
  108.2 32.5 all-gather.10
  143.1 244.8 reduce-scatter.1
  389.6 62.3 all-gather.12
  454.0 27.9 all-gather.8
  483.4 27.3 all-gather.14
where the time goes:
time: 531 us; the launch traced here: 530 us
  waiting for transfers between devices  443 us (83%)
  matrix products  37.5 us (7%)
  local copies, waits for them, and re-layouts  26.8 us (5%)
  between operations  14.2 us (3%)
  other arithmetic  8.65 us (2%)
    reduce_scatter x1, waiting for transfers between devices, per_device(): lax.psum_scatter(partial_value, 'rep', scatter_dimension=0, tiled=True)  246 us
    all_gather x1, waiting for transfers between devices, per_device(): lax.all_gather(ref_qkv, 'fsdp', axis=0, tiled=True)  97.9 us
    all_gather x1, waiting for transfers between devices, per_device(): outer = lax.all_gather(inner, 'fsdp', axis=0, tiled=True)  58.1 us
    all_gather x1, waiting for transfers between devices, per_device(): lax.all_gather(my_keys, 'rep', axis=0, tiled=True)  19.2 us
    all_gather x1, waiting for transfers between devices, per_device(): lax.all_gather(my_vals, 'rep', axis=0, tiled=True)  16.7 us
    reshape x1, local copies, waits for them, and re-layouts, per_device(): partial_value = partial_value.reshape(rows, groups, share + 2, HD)  15.2 us
    dot_general x1, matrix products, per_device(): jnp.dot(tokens, lax.all_gather(ref_qkv, 'fsdp', axis=0, tiled=True), pref...  15.2 us
    sub x1, matrix products, per_device(): expo = jnp.exp(scores - top)  12.1 us
  transfers between devices with their start and end apart: 6, of which 6 were waited for; matrix products, arithmetic and copies ran while one was open for 11% of the time, Pallas kernels for 0%

commit v1 on v0

--- a/solution.py
+++ b/solution.py
@@ -71,7 +71,12 @@
     context = jnp.einsum("hgqk,khd->qhgd", weights, vals, preferred_element_type=jnp.float32)
     context = context.astype(jnp.bfloat16).reshape(mine, groups * share * HD)
     inner = lax.all_gather(policy_key, "rep", axis=0, tiled=True)
-    outer = lax.all_gather(inner, "fsdp", axis=0, tiled=True)
+    ring = [inner]
+    for hop in range(3):
+        ring.append(lax.ppermute(ring[-1], "fsdp", [(dev, (dev + 1) % 4) for dev in range(4)]))
+    outer = jnp.roll(
+        jnp.concatenate(ring[::-1], axis=0), (lax.axis_index("fsdp") + 1) * ring[0].shape[0], axis=0
+    )
     blocks = policy_key.shape[0]
     shards = outer.shape[0] // (blocks * replicas)
     whole = (

time: 531 us -> 471 us (0.89)
  waiting for transfers between devices: 443 us -> 365 us
  local copies, waits for them, and re-layouts: 26.8 us -> 42.8 us
    reduce_scatter x1, waiting for transfers between devices: 246 us -> 150 us  [per_device(): lax.psum_scatter(partial_value, 'rep', scatter_dimension=0, tiled=True)]
    ppermute x0 -> x3, waiting for transfers between devices: none -> 86.4 us  [per_device(): lax.ppermute(ring[-1], 'fsdp', [(dev, (dev + 1) % 4) for dev in range(4)])]
    all_gather x1 -> x0, waiting for transfers between devices: 58.1 us -> none  [per_device(): outer = lax.all_gather(inner, 'fsdp', axis=0, tiled=True)]
    unnamed x11 -> x20, local copies, waits for them, and re-layouts: 4.22 us -> 17.6 us
    all_gather x1, waiting for transfers between devices: 19.2 us -> 9.45 us  [per_device(): lax.all_gather(my_keys, 'rep', axis=0, tiled=True)]
  transfers between devices with their start and end apart: 6 -> 8, of which waited for: 6 -> 8; matrix products, arithmetic and copies ran while one was open for 11% -> 15% of each run, Pallas kernels for 0% -> 0%
where the time goes in v1:
time: 471 us
  waiting for transfers between devices  365 us (77%)
  local copies, waits for them, and re-layouts  42.8 us (9%)
  matrix products  37.5 us (8%)
  between operations  13.9 us (3%)
  other arithmetic  8.52 us (2%)
    reduce_scatter x1, waiting for transfers between devices, per_device(): lax.psum_scatter(partial_value, 'rep', scatter_dimension=0, tiled=True)  150 us
    all_gather x1, waiting for transfers between devices, per_device(): lax.all_gather(ref_qkv, 'fsdp', axis=0, tiled=True)  97.9 us
    ppermute x3, waiting for transfers between devices, per_device(): lax.ppermute(ring[-1], 'fsdp', [(dev, (dev + 1) % 4) for dev in range(4)])  86.4 us
    unnamed x20, local copies, waits for them, and re-layouts  17.6 us
    all_gather x1, waiting for transfers between devices, per_device(): lax.all_gather(my_vals, 'rep', axis=0, tiled=True)  16.7 us
    reshape x1, local copies, waits for them, and re-layouts, per_device(): partial_value = partial_value.reshape(rows, groups, share + 2, HD)  15.2 us
    dot_general x1, matrix products, per_device(): jnp.dot(tokens, lax.all_gather(ref_qkv, 'fsdp', axis=0, tiled=True), pref...  15.2 us
    sub x1, matrix products, per_device(): expo = jnp.exp(scores - top)  12.1 us
  transfers between devices with their start and end apart: 8, of which 8 were waited for; matrix products, arithmetic and copies ran while one was open for 15% of the time, Pallas kernels for 0%

profile of v1, /device:TPU:0, one launch (start us, length us, event | category | flops | bytes accessed | tf_op | source)
XLA Modules:
  0.0 470.5 jit_solution(8207682655184086886)
XLA Ops:
  7.2 0.0 copy-start
  7.2 0.0 all-gather.6.cloned.1.call-start
  7.2 0.7 all-gather.6.cloned.1.call-update
  7.9 0.0 all-gather.10.cloned.1.call-start
  8.0 0.7 all-gather.10.cloned.1.call-update
  8.7 0.0 reduce-scatter.2.cloned.1.call-start
  8.7 97.9 %all-gather.6.cloned.1.call-done = bf16[1280,3584]{1,0:T(8,128)(2,1)} async-done(((bf16[320,3584]{1,0:T(8,128)(2,1)}), bf16[1280,3584]{1,0:T(8,128)(2,1)}) %all-gather.6.cloned.1.call-update) | async-done | bytes 9175056 | tf_op jit(solution)/shard_map/all_gather | solution.py:43
  106.6 0.0 copy-done
  106.6 15.2 %fusion.29 = f32[1024,3584]{0,1:T(8,128)} fusion(bf16[1024,1280]{1,0:T(8,128)(2,1)S(1)} %copy-done, bf16[1280,3584]{1,0:T(8,128)(2,1)} %all-gather.6.cloned.1.call-done), kind=kOutput, calls=%fused_computation.51 | convolution fusion | flops 9395240960 | bytes 26476544 | tf_op jit(solution)/shard_map/dot_general | solution.py:41
  121.8 15.2 %copy.17 = f32[1024,4,7,128]{3,0,2,1:T(8,128)} copy(f32[1024,4,7,128]{0,3,2,1:T(8,128)} %bitcast.54) | data formatting | bytes 29360128 | tf_op jit(solution)/shard_map/reshape | solution.py:46
  137.0 0.0 copy-start.5
  137.0 0.0 copy-start.4
  137.0 0.0 reduce-scatter.2.cloned.1.call-update
  137.0 0.0 all-gather.8.cloned.1.call-start
  137.0 3.7 all-gather.10.cloned.1.call-done
  140.7 1.5 collective-permute-start
  142.2 29.4 %collective-permute-done = bf16[1280,512]{1,0:T(8,128)(2,1)S(1)} collective-permute-done((bf16[1280,512]{1,0:T(8,128)(2,1)}, bf16[1280,512]{1,0:T(8,128)(2,1)S(1)}, u32[]{:S(2)}, u32[]{:S(2)}) %collective-permute-start) | collective-permute-done | bytes 1310752 | tf_op jit(solution)/shard_map/ppermute | solution.py:76
  171.6 0.6 collective-permute-start.1
  172.2 0.0 copy-done.5
  172.2 0.0 copy-done.4
  172.2 0.1 compare_reduce_fusion
  172.3 29.3 %collective-permute-done.1 = bf16[1280,512]{1,0:T(8,128)(2,1)} collective-permute-done((bf16[1280,512]{1,0:T(8,128)(2,1)S(1)}, bf16[1280,512]{1,0:T(8,128)(2,1)}, u32[]{:S(2)}, u32[]{:S(2)}) %collective-permute-start.1) | collective-permute-done | bytes 1310752 | tf_op jit(solution)/shard_map/ppermute | solution.py:76
  201.6 0.0 collective-permute-start.2
  201.6 0.1 add_select_fusion
  201.7 0.3 reduce-window.9
  202.0 0.1 slice.42
  202.1 0.1 slice_reduce_fusion
  202.2 0.1 bitcast_subtract_fusion
  202.3 0.1 dynamic-slice_convert_fusion
  202.4 0.5 multiply_cosine_fusion
  202.9 0.3 fusion.17
  203.2 0.0 copy-start.3
  203.2 27.7 %collective-permute-done.2 = bf16[1280,512]{1,0:T(8,128)(2,1)} collective-permute-done((bf16[1280,512]{1,0:T(8,128)(2,1)}, bf16[1280,512]{1,0:T(8,128)(2,1)}, u32[]{:S(2)}, u32[]{:S(2)}) %collective-permute-start.2) | collective-permute-done | bytes 1310752 | tf_op jit(solution)/shard_map/ppermute | solution.py:76
  230.9 2.5 constant_dynamic-update-slice_fusion.7
  233.4 2.5 constant_dynamic-update-slice_fusion.6
  235.9 1.2 constant_dynamic-update-slice_fusion.5
  237.0 0.0 copy-done.3
  237.0 1.2 constant_dynamic-update-slice_fusion.4
  238.2 149.8 %reduce-scatter.2.cloned.1.call-done = f32[256,4,7,128]{3,0,2,1:T(8,128)} async-done(((f32[1024,4,7,128]{3,0,2,1:T(8,128)}), f32[256,4,7,128]{3,0,2,1:T(8,128)}) %reduce-scatter.2.cloned.1.call-update) | async-done | bytes 3670032 | tf_op jit(solution)/shard_map/reduce_scatter | solution.py:52
  387.9 2.5 broadcast_add_fusion
  390.4 0.0 copy-start.2
  390.4 1.8 copy-done.2
  392.2 0.3 subtract_convert_fusion.1
  392.5 0.9 pad_maximum_fusion.1
  393.3 0.0 all-gather.8.cloned.1.call-update
  393.4 0.2 all-gather.12.cloned.1.call-start
  393.6 2.5 constant_dynamic-update-slice_fusion.3
  396.1 2.5 constant_dynamic-update-slice_fusion.2
  398.6 1.2 constant_dynamic-update-slice_fusion.1
  399.7 1.2 constant_dynamic-update-slice_fusion
  400.9 4.0 constant_dynamic-slice_fusion
  404.9 2.9 copy.20
  407.8 1.8 slice.67
  409.5 0.0 all-gather.12.cloned.1.call-update
  409.6 3.5 subtract_convert_fusion
  413.1 9.4 %all-gather.8.cloned.1.call-done = bf16[1024,4,128]{2,0,1:T(8,128)(2,1)} async-done(((bf16[256,4,128]{2,0,1:T(8,128)(2,1)}), bf16[1024,4,128]{2,0,1:T(8,128)(2,1)}) %all-gather.8.cloned.1.call-update) | async-done | bytes 1048592 | tf_op jit(solution)/shard_map/all_gather | solution.py:57
  422.5 12.1 %fusion.24 = (f32[4,5,256]{2,1,0:T(8,128)S(1)}, f32[4,5,256,1024]{2,3,1,0:T(8,128)}) fusion(pred[256,1024]{0,1:T(8,128)(4,1)S(1)} %fusion.17, bf16[1024,4,128]{2,0,1:T(8,128)(2,1)} %all-gather.8.cloned.1.call-done, bf16[256,4,5,64]{3,0,2,1:T(8,128)(2,1)S(1)} %get-tuple-element.9, bf16[256,4,5,64]{3,0,2,1:T(8,128)(2,1)S(1)} %get-tuple-element.8), kind=kOutput, calls=%fused_computation.50 | convolution fusion | flops 1365771264 | bytes 23613440 | tf_op jit(solution)/shard_map/sub | solution.py:69
  434.7 16.7 %all-gather.12.cloned.1.call-done = bf16[1024,4,1,128]{3,0,2,1:T(8,128)(2,1)} async-done(((bf16[256,4,1,128]{3,0,2,1:T(8,128)(2,1)}), bf16[1024,4,1,128]{3,0,2,1:T(8,128)(2,1)}) %all-gather.12.cloned.1.call-update) | async-done | bytes 1048592 | tf_op jit(solution)/shard_map/all_gather | solution.py:58
  451.4 0.0 copy-start.1
  451.4 10.2 %fusion.8 = bf16[4,128,5,256]{3,1,2,0:T(8,128)(2,1)} fusion(f32[4,5,256,1024]{2,3,1,0:T(8,128)} %get-tuple-element.15, f32[4,5,256]{2,1,0:T(8,128)S(1)} %get-tuple-element.14, bf16[1024,4,1,128]{3,0,2,1:T(8,128)(2,1)} %all-gather.12.cloned.1.call-done), kind=kOutput, calls=%fused_computation.13 | convolution fusion | flops 1353318400 | bytes 23351296 | tf_op jit(solution)/shard_map/hgqk,khd->qhgd/dot_general | solution.py:71
  461.5 2.4 copy.21
  464.0 0.0 copy-done.1
  (6 shorter events, 0.1 us)
Async XLA Ops:
  7.2 99.4 %copy-start = (bf16[1024,1280]{1,0:T(8,128)(2,1)S(1)}, bf16[1024,1280]{1,0:T(8,128)(2,1)}, u32[]{:S(2)}) copy-start(bf16[1024,1280]{1,0:T(8,128)(2,1)} %param.5) | copy-start | bytes 7864324
  7.2 99.4 %all-gather.6.cloned.1.call-start = ((), (), s32[]{:S(2)}) async-start(), calls=%async_computation.1 | async-start | bytes 11468800 | tf_op jit(solution)/shard_map/all_gather | solution.py:43
  7.9 132.8 %all-gather.10.cloned.1.call-start = ((), (), s32[]{:S(2)}) async-start(), calls=%async_computation.4 | async-start | bytes 1638400 | tf_op jit(solution)/shard_map/all_gather | solution.py:73
  8.7 379.3 %reduce-scatter.2.cloned.1.call-start = ((), (), s32[]{:S(2)}) async-start(), calls=%async_computation.2 | async-start | bytes 18350080 | tf_op jit(solution)/shard_map/reduce_scatter | solution.py:52
  137.0 35.2 %copy-start.5 = (f32[3584]{0:T(1024)S(1)}, f32[3584]{0:T(1024)}, u32[]{:S(2)}) copy-start(f32[3584]{0:T(1024)} %param.7) | copy-start | bytes 43012
  137.0 35.3 %copy-start.4 = (s32[1,1024]{1,0:T(1,128)S(1)}, s32[1,1024]{1,0:T(1,128)}, u32[]{:S(2)}) copy-start(s32[1,1024]{1,0:T(1,128)} %param.8) | copy-start | bytes 12292
  137.0 285.6 %all-gather.8.cloned.1.call-start = ((), (), s32[]{:S(2)}) async-start(), calls=%async_computation.3 | async-start | bytes 1310720 | tf_op jit(solution)/shard_map/all_gather | solution.py:57
  140.7 30.9 %collective-permute-start = (bf16[1280,512]{1,0:T(8,128)(2,1)}, bf16[1280,512]{1,0:T(8,128)(2,1)S(1)}, u32[]{:S(2)}, u32[]{:S(2)}) collective-permute-start(bf16[1280,512]{1,0:T(8,128)(2,1)} %all-gather.10.cloned.1.call-done), channel_id=1, source_target_pairs={{0,8},{8,16},{16,24},{24,0},{1,9},{9,17},{17,25},{25,1},{2,10},{10... | collective-permute-start | bytes 3932168 | tf_op jit(solution)/shard_map/ppermute | solution.py:76
  171.6 30.0 %collective-permute-start.1 = (bf16[1280,512]{1,0:T(8,128)(2,1)S(1)}, bf16[1280,512]{1,0:T(8,128)(2,1)}, u32[]{:S(2)}, u32[]{:S(2)}) collective-permute-start(bf16[1280,512]{1,0:T(8,128)(2,1)S(1)} %collective-permute-done), channel_id=1, source_target_pairs={{0,8},{8,16},{16,24},{24,0},{1,9},{9,17},{17,25},{25,1},{2,10},{10... | collective-permute-start | bytes 3932168 | tf_op jit(solution)/shard_map/ppermute | solution.py:76
  201.6 29.3 %collective-permute-start.2 = (bf16[1280,512]{1,0:T(8,128)(2,1)}, bf16[1280,512]{1,0:T(8,128)(2,1)}, u32[]{:S(2)}, u32[]{:S(2)}) collective-permute-start(bf16[1280,512]{1,0:T(8,128)(2,1)} %collective-permute-done.1), channel_id=1, source_target_pairs={{0,8},{8,16},{16,24},{24,0},{1,9},{9,17},{17,25},{25,1},{2,10},{10... | collective-permute-start | bytes 3932168 | tf_op jit(solution)/shard_map/ppermute | solution.py:76
  203.2 33.8 %copy-start.3 = (bf16[1280,512]{1,0:T(8,128)(2,1)S(1)}, bf16[1280,512]{1,0:T(8,128)(2,1)}, u32[]{:S(2)}) copy-start(bf16[1280,512]{1,0:T(8,128)(2,1)} %all-gather.10.cloned.1.call-done) | copy-start | bytes 3932164
  390.4 1.8 copy-start.2
  393.4 58.0 %all-gather.12.cloned.1.call-start = ((), (), s32[]{:S(2)}) async-start(), calls=%async_computation.5 | async-start | bytes 1310720 | tf_op jit(solution)/shard_map/all_gather | solution.py:58
  451.4 12.6 %copy-start.1 = (bf16[1024,1280]{1,0:T(8,128)(2,1)S(1)}, bf16[1024,1280]{1,0:T(8,128)(2,1)}, u32[]{:S(2)}) copy-start(bf16[1024,1280]{1,0:T(8,128)(2,1)} %param.5) | copy-start | bytes 7864324
Sparse Core Ops, SparseCore 0:
  9.8 96.7 all-gather.5
  108.2 32.5 all-gather.9
  143.1 244.8 reduce-scatter.1
  393.5 29.0 all-gather.7
  424.0 27.3 all-gather.11
